TPU v7x, 32 devices: a whole 2x2x4 slice. The times are simulated.
32 devices in a mesh: tile: 8 (over z, x), sub: 4 (over y, core).
Axes of the slice: x: 2, y: 2, z: 4, core: 2. Of those that a mesh axis runs over, the one named last changes fastest.
Arguments:
- initial_state: float32 [8, 64, 1024], P('tile', None, 'sub'), may hold values from -6 to 6
- cotangent: float32 [8, 64, 1024], P('tile', None, 'sub'), may hold values from -6 to 6
- w_in: bfloat16 [576, 1024], replicated, may hold values from -0.25 to 0.25
- b_in: float32 [1024], replicated, may hold values from -3 to 3
- w_out: bfloat16 [64, 1024], replicated, may hold values from -0.1875 to 0.1875
- edge_flips: int32 [8, 2], P('tile'), may hold values 0 or 1
Outputs:
- final_state: float32 [8, 64, 1024], P('tile', None, 'sub')
- grad_state: float32 [8, 64, 1024], P('tile', None, 'sub')
- grad_w_in: float32 [576, 1024], replicated
- grad_b_in: float32 [1024], replicated
- grad_w_out: float32 [64, 1024], replicated
All inputs are finite; a program needn't handle non-finite values. No bound on the sum of `edge_flips` on one device may be relied on, other than what follows from the above.
Results may differ from a plain program's by a relative error of at most 0.006.
Values may be sent and summed in bfloat16 or wider, within the bound.
A program may use at most 64 MiB of HBM per device.

v0:
```python
import jax
import jax.numpy as jnp
from jax import lax
from jax.sharding import PartitionSpec as P

LEVELS = 64
ROWS = 8
STEPS = 4
TILE_ROW = 4
STEP_SIZE = 0.25


def from_behind(value, axis, by):
    peers = lax.axis_size(axis)
    return lax.ppermute(value, axis, [(i, (i + by) % peers) for i in range(peers)])


def passed_along(value, axis, steps):
    count = lax.axis_size(axis)
    first, last = (max(0, -steps), min(count, count - steps))
    return lax.ppermute(value, axis, [(source, source + steps) for source in range(first, last)])


def level_total(vector):
    return lax.psum(vector, ("tile", "sub"))


def seam_shift():
    sub_count = lax.axis_size("sub")
    return sub_count * TILE_ROW - sub_count + 1


def pad_block(current, flip_north, flip_south, first_sub, last_sub):
    block_width = current.shape[2]
    jump = seam_shift()
    west_col, east_col = [
        from_behind(strip, "tile", offset)
        for strip, offset in ((current[:, :, block_width - 1 :], 1), (current[:, :, :1], -1))
    ]
    extended = jnp.concatenate([west_col, current, east_col], axis=2)
    bottom_row = extended[:, ROWS - 1, :]
    top_row = extended[:, 0, :]
    inner_north, inner_south = [
        passed_along(strip, "sub", offset) for strip, offset in ((bottom_row, 1), (top_row, -1))
    ]
    seam_north, seam_south = [
        from_behind(strip, ("tile", "sub"), offset)
        for strip, offset in ((bottom_row, jump), (top_row, -jump))
    ]
    seam_north = jnp.where(flip_north, seam_north[:, ::-1], seam_north)
    north_row = jnp.where(first_sub, seam_north, inner_north)
    seam_south = jnp.where(flip_south, seam_south[:, ::-1], seam_south)
    south_row = jnp.where(last_sub, seam_south, inner_south)
    return jnp.concatenate([north_row[:, None], extended, south_row[:, None]], axis=1)


def unpad_block(pad_grad, flip_north, flip_south, first_sub, last_sub):
    block_width = pad_grad.shape[2] - 2
    jump = seam_shift()
    extended = pad_grad[:, 1:-1, :]
    north_grad = pad_grad[:, 0, :]
    south_grad = pad_grad[:, -1, :]
    unflip_north = jnp.where(flip_north, north_grad[:, ::-1], north_grad)
    unflip_south = jnp.where(flip_south, south_grad[:, ::-1], south_grad)
    nothing = jnp.zeros_like(north_grad)
    seam_bottom, seam_top = [
        from_behind(strip, ("tile", "sub"), offset)
        for strip, offset in (
            (jnp.where(first_sub, unflip_north, nothing), -jump),
            (jnp.where(last_sub, unflip_south, nothing), jump),
        )
    ]
    inner_bottom, inner_top = [
        passed_along(strip, "sub", offset)
        for strip, offset in (
            (jnp.where(first_sub, nothing, north_grad), -1),
            (jnp.where(last_sub, nothing, south_grad), 1),
        )
    ]
    extended = extended.at[:, ROWS - 1, :].add(seam_bottom + inner_bottom)
    extended = extended.at[:, 0, :].add(seam_top + inner_top)
    inner = extended[:, :, 1:-1]
    from_west, from_east = [
        from_behind(strip, "tile", offset)
        for strip, offset in ((extended[:, :, 0], -1), (extended[:, :, -1], 1))
    ]
    inner = inner.at[:, :, block_width - 1].add(from_west)
    inner = inner.at[:, :, 0].add(from_east)
    return inner


def gather_patches(padded, block_width):
    pieces = [
        padded[:, row_shift : row_shift + ROWS, col_shift : col_shift + block_width]
        for row_shift in range(3)
        for col_shift in range(3)
    ]
    return jnp.stack(pieces, axis=0).reshape(9 * LEVELS, ROWS * block_width)


def scatter_patches(patch_grad, block_width):
    pieces = patch_grad.reshape(9, LEVELS, ROWS, block_width)
    total = jnp.zeros((LEVELS, ROWS + 2, block_width + 2), jnp.float32)
    for row_shift in range(3):
        for col_shift in range(3):
            total = total + jnp.pad(
                pieces[3 * row_shift + col_shift],
                ((0, 0), (row_shift, 2 - row_shift), (col_shift, 2 - col_shift)),
            )
    return total


def shards(initial_state, cotangent, w_in, b_in, w_out, edge_flips):
    block_width = initial_state.shape[2] // ROWS
    total_cols = lax.axis_size("tile") * lax.axis_size("sub") * initial_state.shape[2]
    sub_index = lax.axis_index("sub")
    first_sub = sub_index == 0
    last_sub = sub_index == lax.axis_size("sub") - 1
    flip_north = edge_flips[0, 0] == 1
    flip_south = edge_flips[0, 1] == 1

    def network_input(current):
        padded = pad_block(
            current.astype(jnp.bfloat16), flip_north, flip_south, first_sub, last_sub
        )
        return gather_patches(padded, block_width)

    def first_layer(patch_vals):
        product = lax.dot_general(
            w_in, patch_vals, (((0,), (0,)), ((), ())), preferred_element_type=jnp.float32
        )
        return product + b_in[:, None]

    current = initial_state[0].reshape(LEVELS, ROWS, block_width)
    saved_fields = []
    for step_index in range(STEPS):
        saved_fields.append(current)
        patch_vals = network_input(current)
        pre_act = first_layer(patch_vals)
        hidden_vals = jax.nn.silu(pre_act).astype(jnp.bfloat16)
        tendency = jnp.dot(w_out, hidden_vals, preferred_element_type=jnp.float32)
        level_mean = level_total(jnp.sum(tendency, axis=1)) / total_cols
        current = current + (STEP_SIZE * (tendency - level_mean[:, None])).reshape(current.shape)
    gradient = cotangent[0]
    grad_w_in = jnp.zeros((w_in.shape[0], w_in.shape[1]), jnp.float32)
    grad_w_out = jnp.zeros((w_out.shape[0], w_out.shape[1]), jnp.float32)
    grad_b_in = jnp.zeros((w_in.shape[1],), jnp.float32)
    for step_index in reversed(range(STEPS)):
        scaled = STEP_SIZE * gradient
        level_grad = level_total(jnp.sum(scaled, axis=1)) / total_cols
        tend_grad = (scaled - level_grad[:, None]).astype(jnp.bfloat16)
        patch_vals = network_input(saved_fields[step_index])
        pre_act = first_layer(patch_vals)
        hidden_vals = jax.nn.silu(pre_act).astype(jnp.bfloat16)
        grad_w_out = grad_w_out + lax.dot_general(
            tend_grad, hidden_vals, (((1,), (1,)), ((), ())), preferred_element_type=jnp.float32
        )
        hidden_grad = lax.dot_general(
            w_out, tend_grad, (((0,), (0,)), ((), ())), preferred_element_type=jnp.float32
        )
        sigmoid_vals = jax.nn.sigmoid(pre_act)
        pre_grad = hidden_grad * sigmoid_vals * (1.0 + pre_act * (1.0 - sigmoid_vals))
        grad_b_in = grad_b_in + jnp.sum(pre_grad, axis=1)
        pre_low = pre_grad.astype(jnp.bfloat16)
        grad_w_in = grad_w_in + lax.dot_general(
            patch_vals, pre_low, (((1,), (1,)), ((), ())), preferred_element_type=jnp.float32
        )
        patch_grad = jnp.dot(w_in, pre_low, preferred_element_type=jnp.float32)
        pad_grad = scatter_patches(patch_grad, block_width)
        back_grad = unpad_block(pad_grad, flip_north, flip_south, first_sub, last_sub)
        gradient = gradient + back_grad.reshape(LEVELS, ROWS * block_width)
    quarters = (
        lax.psum_scatter(grad_w_in, "sub", scatter_dimension=1, tiled=True),
        lax.psum_scatter(grad_w_out, "sub", scatter_dimension=1, tiled=True),
        lax.psum_scatter(grad_b_in[None, :], "sub", scatter_dimension=1, tiled=True),
    )
    quarters = lax.psum((quarters[0], quarters[1], quarters[2]), "tile")
    grad_w_in, grad_w_out, bias_row = (
        lax.all_gather(quarters[0].astype(jnp.bfloat16), "sub", axis=1, tiled=True).astype(
            jnp.float32
        ),
        lax.all_gather(quarters[1].astype(jnp.bfloat16), "sub", axis=1, tiled=True).astype(
            jnp.float32
        ),
        lax.all_gather(quarters[2].astype(jnp.bfloat16), "sub", axis=1, tiled=True).astype(
            jnp.float32
        ),
    )
    grad_b_in = bias_row[0]
    final_block = current.reshape(1, LEVELS, ROWS * block_width)
    return (final_block, gradient[None], grad_w_in, grad_b_in, grad_w_out)


def solution(mesh):
    in_specs = (P("tile", None, "sub"), P("tile", None, "sub"), P(), P(), P(), P("tile", None))
    out_specs = (P("tile", None, "sub"), P("tile", None, "sub"), P(), P(), P())
    return jax.shard_map(shards, mesh=mesh, in_specs=in_specs, out_specs=out_specs, check_vma=False)
```

profile of v0, /device:TPU:0, one launch (start us, length us, event | category | flops | bytes accessed | tf_op | source)
XLA Modules:
  0.0 664.1 jit_solution(16025712312118512564)
XLA Ops:
  8.3 3.0 collective-permute-start
  11.3 3.1 collective-permute-start.1
  17.3 3.3 collective-permute-start.4
  23.2 2.2 collective-permute-start.3
  26.8 3.6 collective-permute-done.2
  33.8 40.8 %psum.77 = f32[64]{0:T(128)S(1)} all-reduce(f32[64]{0:T(128)S(1)} %get-tuple-element.323), channel_id=1, replica_groups=mesh['tile'=8,'sub'=4] {'tile','sub'}, use_global_device_ids=true, to_apply=%region_1.2 | all-reduce | flops 64 | bytes 512 | tf_op jit(solution)/shard_map/psum | solution.py:25
  75.3 2.3 collective-permute-start.6
  77.7 2.4 collective-permute-start.7
  83.1 4.1 collective-permute-start.9
  87.2 3.2 collective-permute-start.8
  90.5 1.6 collective-permute-done.8
  96.3 42.1 %psum.78 = f32[64]{0:T(128)S(1)} all-reduce(f32[64]{0:T(128)S(1)} %get-tuple-element.327), channel_id=1, replica_groups=mesh['tile'=8,'sub'=4] {'tile','sub'}, use_global_device_ids=true, to_apply=%region_3.4 | all-reduce | flops 64 | bytes 512 | tf_op jit(solution)/shard_map/psum | solution.py:25
  139.0 2.3 collective-permute-start.12
  141.3 2.4 collective-permute-start.13
  146.7 1.7 collective-permute-start.16
  150.0 3.6 collective-permute-start.14
  158.4 43.7 %all-reduce.37 = (f32[64]{0:T(128)S(1)}, f32[64]{0:T(128)S(1)}) all-reduce(f32[64]{0:T(128)S(1)} %get-tuple-element.331, f32[64]{0:T(128)S(1)} %fusion.26), channel_id=1, replica_groups=mesh['tile'=8,'sub'=4] {'tile','sub'}, use_global_device_ids=true, to_apply=%region_5.6 | all-reduce | flops 128 | bytes 1024 | tf_op jit(solution)/shard_map/psum | solution.py:25
  202.3 2.3 collective-permute-start.18
  204.6 2.4 collective-permute-start.19
  210.0 3.8 collective-permute-start.21
  213.9 3.7 collective-permute-start.20
  248.1 2.1 fusion.45
  250.2 3.2 collective-permute-start.27
  253.3 3.6 collective-permute-start.26
  257.0 2.3 collective-permute-done.26
  259.3 4.2 collective-permute-start.28
  265.3 6.3 collective-permute-done.29
  272.3 36.8 %psum.82 = f32[64]{0:T(128)S(1)} all-reduce(f32[64]{0:T(128)S(1)} %get-tuple-element.214), channel_id=1, replica_groups=mesh['tile'=8,'sub'=4] {'tile','sub'}, use_global_device_ids=true, to_apply=%region_11.12 | all-reduce | flops 64 | bytes 512 | tf_op jit(solution)/shard_map/psum | solution.py:25
  309.1 1.9 fusion.78
  323.5 1.6 copy.210
  325.1 1.6 copy.209
  333.0 2.9 collective-permute-start.30
  337.3 3.0 fusion.17
  340.3 4.5 collective-permute-start.33
  345.7 4.2 collective-permute-done.32
  350.5 1.6 scatter-add.61
  352.8 1.6 collective-permute-start.34
  354.4 1.7 copy_add_fusion.1
  358.9 4.5 collective-permute-done.35
  365.8 36.9 %psum.83 = f32[64]{0:T(128)} all-reduce(f32[64]{0:T(128)S(1)} %multiply_reduce_fusion.1), channel_id=1, replica_groups=mesh['tile'=8,'sub'=4] {'tile','sub'}, use_global_device_ids=true, to_apply=%region_13.14 | all-reduce | flops 64 | bytes 512 | tf_op jit(solution)/shard_map/psum | solution.py:25
  404.4 2.4 fusion.76
  408.2 1.6 copy.224
  413.0 1.6 copy.230
  428.9 2.9 collective-permute-start.36
  434.5 4.4 collective-permute-start.39
  439.7 4.2 collective-permute-done.38
  444.6 1.9 collective-permute-start.40
  449.6 5.1 collective-permute-done.41
  458.0 37.1 %all-reduce.36 = (f32[64]{0:T(128)}, f32[64]{0:T(128)}) all-reduce(f32[64]{0:T(128)} %get-tuple-element.335, f32[64]{0:T(128)S(1)} %multiply_reduce_fusion), channel_id=1, replica_groups=mesh['tile'=8,'sub'=4] {'tile','sub'}, use_global_device_ids=true, to_apply=%region_7.8 | all-reduce | flops 128 | bytes 1024 | tf_op jit(solution)/shard_map/psum | solution.py:25
  496.8 2.6 fusion.75
  500.6 2.1 convolution_add_fusion.4
  502.7 1.8 fusion.14
  504.8 2.0 add_add_fusion
  509.7 2.8 collective-permute-start.42
  513.7 9.6 %reduce-scatter.10.cloned.1.call-done = f32[256,1]{1,0:T(8,128)} async-done(((f32[1024,1]{1,0:T(8,128)}), f32[256,1]{1,0:T(8,128)}) %reduce-scatter.10.cloned.1.call-update) | async-done | bytes 1040
  524.3 21.9 %reduce-scatter.8.cloned.1.call-done = f32[64,256]{1,0:T(8,128)} async-done(((f32[64,1024]{1,0:T(8,128)}), f32[64,256]{1,0:T(8,128)}) %reduce-scatter.8.cloned.1.call-update) | async-done | bytes 65552 | tf_op jit(solution)/shard_map/reduce_scatter | solution.py:174
  546.2 35.9 %reduce-scatter.6.cloned.1.call-done = f32[576,256]{1,0:T(8,128)} async-done(((f32[576,1024]{1,0:T(8,128)}), f32[576,256]{1,0:T(8,128)}) %reduce-scatter.6.cloned.1.call-update) | async-done | bytes 589840 | tf_op jit(solution)/shard_map/reduce_scatter | solution.py:173
  582.1 44.4 %all-reduce.40 = (bf16[576,256]{1,0:T(8,128)(2,1)}, bf16[1,256]{1,0:T(2,128)(2,1)S(1)}, bf16[64,256]{1,0:T(8,128)(2,1)S(1)}) all-reduce(f32[576,256]{1,0:T(8,128)} %reduce-scatter.6.cloned.1.call-done, f32[1,256]{1,0:T(1,128)S(1)} %copy.248, f32[64,256]{1,0:T(8,128)} %reduce-scatter.8.cloned.1.call-done), channel_id=1, replica_groups=mesh['tile'=8,'sub'=4] {'tile'}, use_global_device_ids=true, to_apply=%region_17.18 | all-reduce | flops 164096 | bytes 984576 | tf_op jit(solution)/shard_map/psum | solution.py:177
  628.7 4.2 collective-permute-done.44
  632.9 1.9 collective-permute-start.46
  636.6 5.3 collective-permute-done.47
  642.8 5.1 all_gather.10
  648.5 5.4 all_gather.11
  654.6 3.0 convert_element_type.174
  (397 shorter events, 135.9 us)
Async XLA Ops:
  7.2 516.1 %reduce-scatter.10.cloned.1.call-start = ((), (), s32[]{:S(2)}) async-start(), calls=%async_computation.6 | async-start | bytes 655360
  8.3 7.6 %collective-permute-start = (bf16[64,8,1]{0,2,1:T(2,128)(2,1)S(1)}, bf16[64,8,1]{0,2,1:T(2,128)(2,1)S(1)}, u32[]{:S(2)}, u32[]{:S(2)}) collective-permute-start(bf16[64,8,1]{0,2,1:T(2,128)(2,1)S(1)} %get-tuple-element.317), channel_id=1, source_target_pairs={{0,4},{4,8},{8,12},{12,16},{16,20},{20,24},{24,28},{28,0},{1,5},{5... | collective-permute-start | bytes 3080 | tf_op jit(solution)/shard_map/ppermute | solution.py:15
  11.3 4.6 collective-permute-start.1
  16.0 10.8 %collective-permute-start.5 = (bf16[64,34]{0,1:T(8,128)(2,1)S(1)}, bf16[64,34]{0,1:T(8,128)(2,1)S(1)}, u32[]{:S(2)}, u32[]{:S(2)}) collective-permute-start(bf16[64,34]{0,1:T(8,128)(2,1)S(1)} %get-tuple-element.309), channel_id=1, source_target_pairs={{1,0},{2,1},{3,2},{5,4},{6,5},{7,6},{9,8},{10,9},{11,10},{13,12},{... | collective-permute-start | bytes 13064 | tf_op jit(solution)/shard_map/ppermute | solution.py:21
  17.3 9.5 %collective-permute-start.4 = (bf16[64,34]{0,1:T(8,128)(2,1)S(1)}, bf16[64,34]{0,1:T(8,128)(2,1)S(1)}, u32[]{:S(2)}, u32[]{:S(2)}) collective-permute-start(bf16[64,34]{0,1:T(8,128)(2,1)S(1)} %get-tuple-element.309), channel_id=1, source_target_pairs={{0,19},{1,20},{2,21},{3,22},{4,23},{5,24},{6,25},{7,26},{8,27},{9,... | collective-permute-start | bytes 13064 | tf_op jit(solution)/shard_map/ppermute | solution.py:15
  23.2 7.2 %collective-permute-start.3 = (bf16[64,34]{0,1:T(8,128)(2,1)S(1)}, bf16[64,34]{0,1:T(8,128)(2,1)S(1)}, u32[]{:S(2)}, u32[]{:S(2)}) collective-permute-start(bf16[64,34]{0,1:T(8,128)(2,1)S(1)} %get-tuple-element.310), channel_id=1, source_target_pairs={{0,1},{1,2},{2,3},{4,5},{5,6},{6,7},{8,9},{9,10},{10,11},{12,13},{... | collective-permute-start | bytes 13064 | tf_op jit(solution)/shard_map/ppermute | solution.py:21
  25.4 4.9 collective-permute-start.2
  75.3 6.4 collective-permute-start.6
  77.7 4.0 collective-permute-start.7
  81.7 8.7 %collective-permute-start.10 = (bf16[64,34]{0,1:T(8,128)(2,1)S(1)}, bf16[64,34]{0,1:T(8,128)(2,1)S(1)}, u32[]{:S(2)}, u32[]{:S(2)}) collective-permute-start(bf16[64,34]{0,1:T(8,128)(2,1)S(1)} %get-tuple-element.305), channel_id=1, source_target_pairs={{0,19},{1,20},{2,21},{3,22},{4,23},{5,24},{6,25},{7,26},{8,27},{9,... | collective-permute-start | bytes 13064 | tf_op jit(solution)/shard_map/ppermute | solution.py:15
  81.8 8.7 %collective-permute-start.11 = (bf16[64,34]{0,1:T(8,128)(2,1)S(1)}, bf16[64,34]{0,1:T(8,128)(2,1)S(1)}, u32[]{:S(2)}, u32[]{:S(2)}) collective-permute-start(bf16[64,34]{0,1:T(8,128)(2,1)S(1)} %get-tuple-element.305), channel_id=1, source_target_pairs={{1,0},{2,1},{3,2},{5,4},{6,5},{7,6},{9,8},{10,9},{11,10},{13,12},{... | collective-permute-start | bytes 13064 | tf_op jit(solution)/shard_map/ppermute | solution.py:21
  83.1 9.1 %collective-permute-start.9 = (bf16[64,34]{0,1:T(8,128)(2,1)S(1)}, bf16[64,34]{0,1:T(8,128)(2,1)S(1)}, u32[]{:S(2)}, u32[]{:S(2)}) collective-permute-start(bf16[64,34]{0,1:T(8,128)(2,1)S(1)} %get-tuple-element.306), channel_id=1, source_target_pairs={{0,1},{1,2},{2,3},{4,5},{5,6},{6,7},{8,9},{9,10},{10,11},{12,13},{... | collective-permute-start | bytes 13064 | tf_op jit(solution)/shard_map/ppermute | solution.py:21
  87.2 4.9 collective-permute-start.8
  139.0 6.4 collective-permute-start.12
  141.3 4.0 collective-permute-start.13
  145.4 8.2 %collective-permute-start.17 = (bf16[64,34]{0,1:T(8,128)(2,1)S(1)}, bf16[64,34]{0,1:T(8,128)(2,1)S(1)}, u32[]{:S(2)}, u32[]{:S(2)}) collective-permute-start(bf16[64,34]{0,1:T(8,128)(2,1)S(1)} %get-tuple-element.301), channel_id=1, source_target_pairs={{1,0},{2,1},{3,2},{5,4},{6,5},{7,6},{9,8},{10,9},{11,10},{13,12},{... | collective-permute-start | bytes 13064 | tf_op jit(solution)/shard_map/ppermute | solution.py:21
  146.7 6.9 %collective-permute-start.16 = (bf16[64,34]{0,1:T(8,128)(2,1)S(1)}, bf16[64,34]{0,1:T(8,128)(2,1)S(1)}, u32[]{:S(2)}, u32[]{:S(2)}) collective-permute-start(bf16[64,34]{0,1:T(8,128)(2,1)S(1)} %get-tuple-element.301), channel_id=1, source_target_pairs={{0,19},{1,20},{2,21},{3,22},{4,23},{5,24},{6,25},{7,26},{8,27},{9,... | collective-permute-start | bytes 13064 | tf_op jit(solution)/shard_map/ppermute | solution.py:15
  148.5 6.5 collective-permute-start.15
  150.0 5.0 collective-permute-start.14
  202.3 6.4 collective-permute-start.18
  204.6 4.0 collective-permute-start.19
  208.7 8.9 %collective-permute-start.22 = (bf16[64,34]{0,1:T(8,128)(2,1)S(1)}, bf16[64,34]{0,1:T(8,128)(2,1)S(1)}, u32[]{:S(2)}, u32[]{:S(2)}) collective-permute-start(bf16[64,34]{0,1:T(8,128)(2,1)S(1)} %get-tuple-element.297), channel_id=1, source_target_pairs={{0,19},{1,20},{2,21},{3,22},{4,23},{5,24},{6,25},{7,26},{8,27},{9,... | collective-permute-start | bytes 13064 | tf_op jit(solution)/shard_map/ppermute | solution.py:15
  208.7 8.9 %collective-permute-start.23 = (bf16[64,34]{0,1:T(8,128)(2,1)S(1)}, bf16[64,34]{0,1:T(8,128)(2,1)S(1)}, u32[]{:S(2)}, u32[]{:S(2)}) collective-permute-start(bf16[64,34]{0,1:T(8,128)(2,1)S(1)} %get-tuple-element.297), channel_id=1, source_target_pairs={{1,0},{2,1},{3,2},{5,4},{6,5},{7,6},{9,8},{10,9},{11,10},{13,12},{... | collective-permute-start | bytes 13064 | tf_op jit(solution)/shard_map/ppermute | solution.py:21
  210.0 9.0 %collective-permute-start.21 = (bf16[64,34]{0,1:T(8,128)(2,1)S(1)}, bf16[64,34]{0,1:T(8,128)(2,1)S(1)}, u32[]{:S(2)}, u32[]{:S(2)}) collective-permute-start(bf16[64,34]{0,1:T(8,128)(2,1)S(1)} %get-tuple-element.298), channel_id=1, source_target_pairs={{0,1},{1,2},{2,3},{4,5},{5,6},{6,7},{8,9},{9,10},{10,11},{12,13},{... | collective-permute-start | bytes 13064 | tf_op jit(solution)/shard_map/ppermute | solution.py:21
  213.9 5.1 collective-permute-start.20
  245.4 11.6 %collective-permute-start.24 = (f32[64,34]{0,1:T(8,128)S(1)}, f32[64,34]{0,1:T(8,128)S(1)}, u32[]{:S(2)}, u32[]{:S(2)}) collective-permute-start(f32[64,34]{0,1:T(8,128)S(1)} %get-tuple-element.279), channel_id=1, source_target_pairs={{0,19},{1,20},{2,21},{3,22},{4,23},{5,24},{6,25},{7,26},{8,27},{9,... | collective-permute-start | bytes 26120 | tf_op jit(solution)/shard_map/ppermute | solution.py:15
  246.8 10.1 %collective-permute-start.25 = (f32[64,34]{0,1:T(8,128)S(1)}, f32[64,34]{0,1:T(8,128)S(1)}, u32[]{:S(2)}, u32[]{:S(2)}) collective-permute-start(f32[64,34]{0,1:T(8,128)S(1)} %get-tuple-element.280), channel_id=1, source_target_pairs={{1,0},{2,1},{3,2},{5,4},{6,5},{7,6},{9,8},{10,9},{11,10},{13,12},{... | collective-permute-start | bytes 26120 | tf_op jit(solution)/shard_map/ppermute | solution.py:21
  250.2 6.8 %collective-permute-start.27 = (f32[64,34]{0,1:T(8,128)S(1)}, f32[64,34]{0,1:T(8,128)S(1)}, u32[]{:S(2)}, u32[]{:S(2)}) collective-permute-start(f32[64,34]{0,1:T(8,128)S(1)} %get-tuple-element.278), channel_id=1, source_target_pairs={{0,1},{1,2},{2,3},{4,5},{5,6},{6,7},{8,9},{9,10},{10,11},{12,13},{... | collective-permute-start | bytes 26120 | tf_op jit(solution)/shard_map/ppermute | solution.py:21
  253.3 6.0 collective-permute-start.26
  259.3 5.9 collective-permute-start.28
  265.2 6.4 collective-permute-start.29
  333.0 12.0 %collective-permute-start.30 = (f32[64,34]{0,1:T(8,128)S(1)}, f32[64,34]{0,1:T(8,128)S(1)}, u32[]{:S(2)}, u32[]{:S(2)}) collective-permute-start(f32[64,34]{0,1:T(8,128)S(1)} %get-tuple-element.273), channel_id=1, source_target_pairs={{0,19},{1,20},{2,21},{3,22},{4,23},{5,24},{6,25},{7,26},{8,27},{9,... | collective-permute-start | bytes 26120 | tf_op jit(solution)/shard_map/ppermute | solution.py:15
  335.8 9.1 %collective-permute-start.31 = (f32[64,34]{0,1:T(8,128)S(1)}, f32[64,34]{0,1:T(8,128)S(1)}, u32[]{:S(2)}, u32[]{:S(2)}) collective-permute-start(f32[64,34]{0,1:T(8,128)S(1)} %get-tuple-element.274), channel_id=1, source_target_pairs={{1,0},{2,1},{3,2},{5,4},{6,5},{7,6},{9,8},{10,9},{11,10},{13,12},{... | collective-permute-start | bytes 26120 | tf_op jit(solution)/shard_map/ppermute | solution.py:21
  340.3 5.4 collective-permute-start.33
  344.8 5.1 collective-permute-start.32
  352.8 4.7 collective-permute-start.34
  357.1 6.4 collective-permute-start.35
  428.9 10.7 %collective-permute-start.36 = (f32[64,34]{0,1:T(8,128)S(1)}, f32[64,34]{0,1:T(8,128)S(1)}, u32[]{:S(2)}, u32[]{:S(2)}) collective-permute-start(f32[64,34]{0,1:T(8,128)S(1)} %get-tuple-element.267), channel_id=1, source_target_pairs={{0,19},{1,20},{2,21},{3,22},{4,23},{5,24},{6,25},{7,26},{8,27},{9,... | collective-permute-start | bytes 26120 | tf_op jit(solution)/shard_map/ppermute | solution.py:15
  431.8 7.8 %collective-permute-start.37 = (f32[64,34]{0,1:T(8,128)S(1)}, f32[64,34]{0,1:T(8,128)S(1)}, u32[]{:S(2)}, u32[]{:S(2)}) collective-permute-start(f32[64,34]{0,1:T(8,128)S(1)} %get-tuple-element.268), channel_id=1, source_target_pairs={{1,0},{2,1},{3,2},{5,4},{6,5},{7,6},{9,8},{10,9},{11,10},{13,12},{... | collective-permute-start | bytes 26120 | tf_op jit(solution)/shard_map/ppermute | solution.py:21
  434.5 5.2 collective-permute-start.39
  438.9 5.1 collective-permute-start.38
  444.6 3.6 collective-permute-start.40
  448.1 6.6 collective-permute-start.41
  500.5 45.7 %reduce-scatter.8.cloned.1.call-start = ((), (), s32[]{:S(2)}) async-start(), calls=%async_computation.5 | async-start | bytes 327680 | tf_op jit(solution)/shard_map/reduce_scatter | solution.py:174
  502.7 79.4 %reduce-scatter.6.cloned.1.call-start = ((), (), s32[]{:S(2)}) async-start(), calls=%async_computation.3 | async-start | bytes 2949120 | tf_op jit(solution)/shard_map/reduce_scatter | solution.py:173
  506.8 147.8 %all-gather.2.cloned.1.call-start = ((), (), s32[]{:S(2)}) async-start(), calls=%async_computation.4 | async-start | bytes 1474560 | tf_op jit(solution)/shard_map/all_gather | solution.py:179
  509.3 117.2 %copy-start.53 = (f32[64]{0:T(128)S(1)}, f32[64]{0:T(128)}, u32[]{:S(2)}) copy-start(f32[64]{0:T(128)} %get-tuple-element.207) | copy-start | bytes 772
  509.5 125.3 %copy-start.34 = (f32[256,64]{0,1:T(8,128)S(1)}, f32[256,64]{0,1:T(8,128)}, u32[]{:S(2)}) copy-start(f32[256,64]{0,1:T(8,128)} %copy-done.33) | copy-start | bytes 196612
  509.5 125.3 %copy-start.36 = (f32[256,64]{0,1:T(8,128)S(1)}, f32[256,64]{0,1:T(8,128)}, u32[]{:S(2)}) copy-start(f32[256,64]{0,1:T(8,128)} %copy-done.35) | copy-start | bytes 196612
  509.5 125.3 %copy-start.38 = (f32[256,64]{0,1:T(8,128)S(1)}, f32[256,64]{0,1:T(8,128)}, u32[]{:S(2)}) copy-start(f32[256,64]{0,1:T(8,128)} %copy-done.37) | copy-start | bytes 196612
  509.5 125.3 %copy-start.41 = (f32[1,64,256]{2,1,0:T(8,128)S(1)}, f32[1,64,256]{2,1,0:T(8,128)}, u32[]{:S(2)}) copy-start(f32[1,64,256]{2,1,0:T(8,128)} %param.38) | copy-start | bytes 196612
  509.5 125.3 %copy-start.42 = (f32[256,64]{0,1:T(8,128)S(1)}, f32[256,64]{0,1:T(8,128)}, u32[]{:S(2)}) copy-start(f32[256,64]{0,1:T(8,128)} %get-tuple-element.336) | copy-start | bytes 196612
  509.5 125.3 %copy-start.47 = (f32[64]{0:T(128)S(1)}, f32[64]{0:T(128)}, u32[]{:S(2)}) copy-start(f32[64]{0:T(128)} %copy-done.46) | copy-start | bytes 772
  509.6 125.3 %copy-start.49 = (f32[64]{0:T(128)S(1)}, f32[64]{0:T(128)}, u32[]{:S(2)}) copy-start(f32[64]{0:T(128)} %copy-done.48) | copy-start | bytes 772
  509.6 132.4 %copy-start.4 = (f32[1,64,256]{1,2,0:T(8,128)S(1)}, f32[1,64,256]{1,2,0:T(8,128)}, u32[]{:S(2)}) copy-start(f32[1,64,256]{1,2,0:T(8,128)} %copy-done.2) | copy-start | bytes 196612
  509.6 132.4 %copy-start.5 = (f32[64,8,32]{0,2,1:T(8,128)S(1)}, f32[64,8,32]{0,2,1:T(8,128)}, u32[]{:S(2)}) copy-start(f32[64,8,32]{0,2,1:T(8,128)} %scatter-add.65) | copy-start | bytes 196612
  509.7 132.4 %copy-start.6 = (f32[64,8,32]{0,2,1:T(8,128)S(1)}, f32[64,8,32]{0,2,1:T(8,128)}, u32[]{:S(2)}) copy-start(f32[64,8,32]{0,2,1:T(8,128)} %scatter-add.71) | copy-start | bytes 196612
  509.7 132.4 %copy-start.26 = (f32[64,8,32]{0,2,1:T(8,128)S(1)}, f32[64,8,32]{0,2,1:T(8,128)}, u32[]{:S(2)}) copy-start(f32[64,8,32]{0,2,1:T(8,128)} %copy-done.25) | copy-start | bytes 196612
  509.7 118.3 %collective-permute-start.42 = (f32[64,34]{0,1:T(8,128)S(1)}, f32[64,34]{0,1:T(8,128)S(1)}, u32[]{:S(2)}, u32[]{:S(2)}) collective-permute-start(f32[64,34]{0,1:T(8,128)S(1)} %get-tuple-element.261), channel_id=1, source_target_pairs={{0,19},{1,20},{2,21},{3,22},{4,23},{5,24},{6,25},{7,26},{8,27},{9,... | collective-permute-start | bytes 26120 | tf_op jit(solution)/shard_map/ppermute | solution.py:15
  512.4 115.5 %collective-permute-start.43 = (f32[64,34]{0,1:T(8,128)S(1)}, f32[64,34]{0,1:T(8,128)S(1)}, u32[]{:S(2)}, u32[]{:S(2)}) collective-permute-start(f32[64,34]{0,1:T(8,128)S(1)} %get-tuple-element.262), channel_id=1, source_target_pairs={{1,0},{2,1},{3,2},{5,4},{6,5},{7,6},{9,8},{10,9},{11,10},{13,12},{... | collective-permute-start | bytes 26120 | tf_op jit(solution)/shard_map/ppermute | solution.py:21
  626.6 2.1 collective-permute-start.45
  627.9 5.1 collective-permute-start.44
  632.9 3.7 collective-permute-start.46
  635.6 6.4 collective-permute-start.47
  (45 other events, 614.7 us)
Sparse Core Ops, SparseCore 0:
  500.6 22.5 reduce-scatter.9
  526.3 19.8 reduce-scatter.7
  549.3 32.7 reduce-scatter.5
  626.6 15.1 all-gather.1
where the time goes:
time: 668 us; the launch traced here: 664 us
  blocking collectives  292 us (44%)
  waiting for transfers between devices  119 us (18%)
  starting transfers between devices  98 us (15%)
  local copies, waits for them, and re-layouts  82.4 us (12%)
  matrix products  32.2 us (5%)
  other arithmetic  23.4 us (4%)
  between operations  16.5 us (2%)
    psum x6, blocking collectives, level_total(): return lax.psum(vector, ('tile', 'sub'))  237 us
    ppermute x32, starting transfers between devices, from_behind(): lax.ppermute(value, axis, [(i, (i + by) % peers) for i in range(peers)])  62.4 us
    ppermute x32, waiting for transfers between devices, from_behind(): lax.ppermute(value, axis, [(i, (i + by) % peers) for i in range(peers)])  51.1 us
    slice x40, local copies, waits for them, and re-layouts, scatter_patches(): pieces[3 * row_shift + col_shift]  46.4 us
    psum x1, blocking collectives, shards(): quarters = lax.psum((quarters[0], quarters[1], quarters[2]), 'tile')  44.4 us
    reduce_scatter x1, waiting for transfers between devices, shards(): lax.psum_scatter(grad_w_in, 'sub', scatter_dimension=1, tiled=True)  35.9 us
    ppermute x16, starting transfers between devices, passed_along(): lax.ppermute(value, axis, [(source, source + steps) for source in range(f...  35.4 us
    reduce_scatter x1, waiting for transfers between devices, shards(): lax.psum_scatter(grad_w_out, 'sub', scatter_dimension=1, tiled=True)  21.9 us
  transfers between devices with their start and end apart: 52, of which 22 were waited for; matrix products, arithmetic and copies ran while one was open for 4% of the time, Pallas kernels for 0%

commit v1 on v0

--- a/solution.py
+++ b/solution.py
@@ -2,6 +2,7 @@
 import jax.numpy as jnp
 from jax import lax
 from jax.sharding import PartitionSpec as P
+from jax.lax import psum
 
 LEVELS = 64
 ROWS = 8
@@ -10,6 +11,12 @@
 STEP_SIZE = 0.25
 
 
+def match_the_plate(a_name, raw, chip_axis):
+    passed = psum(raw, chip_axis)
+    y2 = psum(passed, a_name)
+    return y2
+
+
 def from_behind(value, axis, by):
     peers = lax.axis_size(axis)
     return lax.ppermute(value, axis, [(i, (i + by) % peers) for i in range(peers)])
@@ -22,7 +29,7 @@
 
 
 def level_total(vector):
-    return lax.psum(vector, ("tile", "sub"))
+    return match_the_plate("tile", vector, "sub")
 
 
 def seam_shift():

time: 668 us -> 569 us (0.85)
  blocking collectives: 292 us -> 209 us
  waiting for transfers between devices: 119 us -> 104 us
    psum x7 -> x13, blocking collectives: 282 us -> 198 us  [the longest x7 159 us: match_the_plate(): y2 = psum(passed, a_name)]
    ppermute x32, waiting for transfers between devices: 51.1 us -> 41.6 us  [from_behind(): lax.ppermute(value, axis, [(i, (i + by) % peers) for i in range(peers)])]
  transfers between devices with their start and end apart: 52 -> 52, of which waited for: 22 -> 19; matrix products, arithmetic and copies ran while one was open for 4% -> 5% of each run, Pallas kernels for 0% -> 0%
where the time goes in v1:
time: 569 us; the launch traced here: 565 us
  blocking collectives  209 us (37%)
  waiting for transfers between devices  104 us (18%)
  starting transfers between devices  99.7 us (18%)
  local copies, waits for them, and re-layouts  81.3 us (14%)
  matrix products  32.1 us (6%)
  other arithmetic  22.8 us (4%)
  between operations  16.6 us (3%)
    psum x7, blocking collectives, match_the_plate(): y2 = psum(passed, a_name)  159 us
    ppermute x32, starting transfers between devices, from_behind(): lax.ppermute(value, axis, [(i, (i + by) % peers) for i in range(peers)])  65.4 us
    slice x40, local copies, waits for them, and re-layouts, scatter_patches(): pieces[3 * row_shift + col_shift]  46.4 us
    ppermute x32, waiting for transfers between devices, from_behind(): lax.ppermute(value, axis, [(i, (i + by) % peers) for i in range(peers)])  41.6 us
    psum x6, blocking collectives, match_the_plate(): passed = psum(raw, chip_axis)  38.8 us
    reduce_scatter x1, waiting for transfers between devices, shards(): lax.psum_scatter(grad_w_in, 'sub', scatter_dimension=1, tiled=True)  36 us
    ppermute x16, starting transfers between devices, passed_along(): lax.ppermute(value, axis, [(source, source + steps) for source in range(f...  34.1 us
    reduce_scatter x1, waiting for transfers between devices, shards(): lax.psum_scatter(grad_w_out, 'sub', scatter_dimension=1, tiled=True)  22.1 us
  transfers between devices with their start and end apart: 52, of which 19 were waited for; matrix products, arithmetic and copies ran while one was open for 5% of the time, Pallas kernels for 0%

profile of v1, /device:TPU:0, one launch (start us, length us, event | category | flops | bytes accessed | tf_op | source)
XLA Modules:
  0.0 565.2 jit_solution(7875607571825594358)
XLA Ops:
  8.3 3.0 collective-permute-start
  11.3 3.1 collective-permute-start.1
  17.3 3.3 collective-permute-start.4
  23.2 2.2 collective-permute-start.3
  26.8 3.6 collective-permute-done.2
  33.8 7.9 %psum.133 = f32[64]{0:T(128)S(1)} all-reduce(f32[64]{0:T(128)S(1)} %get-tuple-element.326), channel_id=1, replica_groups=mesh['tile'=8,'sub'=4] {'sub'}, use_global_device_ids=true, to_apply=%region_1.2 | all-reduce | flops 64 | bytes 512 | tf_op jit(solution)/shard_map/psum | solution.py:15
  41.6 18.6 %psum.134 = f32[64]{0:T(128)S(1)} all-reduce(f32[64]{0:T(128)S(1)} %psum.133), channel_id=1, replica_groups=mesh['tile'=8,'sub'=4] {'tile'}, use_global_device_ids=true, to_apply=%region_2.3 | all-reduce | flops 64 | bytes 512 | tf_op jit(solution)/shard_map/psum | solution.py:16
  61.6 4.2 collective-permute-start.7
  68.8 3.0 collective-permute-start.9
  71.9 3.9 collective-permute-start.8
  80.6 6.5 %psum.135 = f32[64]{0:T(128)S(1)} all-reduce(f32[64]{0:T(128)S(1)} %get-tuple-element.330), channel_id=1, replica_groups=mesh['tile'=8,'sub'=4] {'sub'}, use_global_device_ids=true, to_apply=%region_4.5 | all-reduce | flops 64 | bytes 512 | tf_op jit(solution)/shard_map/psum | solution.py:15
  87.1 22.0 %psum.136 = f32[64]{0:T(128)S(1)} all-reduce(f32[64]{0:T(128)S(1)} %psum.135), channel_id=1, replica_groups=mesh['tile'=8,'sub'=4] {'tile'}, use_global_device_ids=true, to_apply=%region_5.6 | all-reduce | flops 64 | bytes 512 | tf_op jit(solution)/shard_map/psum | solution.py:16
  110.0 4.7 collective-permute-start.13
  117.7 3.0 collective-permute-start.15
  120.8 3.8 collective-permute-start.14
  129.3 5.9 %all-reduce.39 = (f32[64]{0:T(128)S(1)}, f32[64]{0:T(128)S(1)}) all-reduce(f32[64]{0:T(128)S(1)} %get-tuple-element.334, f32[64]{0:T(128)S(1)} %fusion.26), channel_id=1, replica_groups=mesh['tile'=8,'sub'=4] {'sub'}, use_global_device_ids=true, to_apply=%region_7.8 | all-reduce | flops 128 | bytes 1024 | tf_op jit(solution)/shard_map/psum | solution.py:15
  135.2 22.6 %all-reduce.37 = (f32[64]{0:T(128)S(1)}, f32[64]{0:T(128)S(1)}) all-reduce(f32[64]{0:T(128)S(1)} %get-tuple-element.215, f32[64]{0:T(128)S(1)} %get-tuple-element.216), channel_id=1, replica_groups=mesh['tile'=8,'sub'=4] {'tile'}, use_global_device_ids=true, to_apply=%region_8.9 | all-reduce | flops 128 | bytes 1024 | tf_op jit(solution)/shard_map/psum | solution.py:16
  158.1 4.7 collective-permute-start.19
  165.8 3.0 collective-permute-start.21
  168.8 4.1 collective-permute-start.20
  183.2 1.6 copy.200
  202.9 2.1 fusion.45
  204.9 3.2 collective-permute-start.27
  208.1 3.1 collective-permute-start.26
  211.2 3.3 collective-permute-done.26
  214.5 4.7 collective-permute-start.28
  221.0 6.3 %collective-permute-done.29 = f32[64,8]{0,1:T(8,128)S(1)} collective-permute-done((f32[64,8]{0,1:T(8,128)S(1)}, f32[64,8]{0,1:T(8,128)S(1)}, u32[]{:S(2)}, u32[]{:S(2)}) %collective-permute-start.29) | collective-permute-done | bytes 2080 | tf_op jit(solution)/shard_map/ppermute | solution.py:22
  228.0 5.7 %psum.143 = f32[64]{0:T(128)S(1)} all-reduce(f32[64]{0:T(128)S(1)} %get-tuple-element.217), channel_id=1, replica_groups=mesh['tile'=8,'sub'=4] {'sub'}, use_global_device_ids=true, to_apply=%region_16.17 | all-reduce | flops 64 | bytes 512 | tf_op jit(solution)/shard_map/psum | solution.py:15
  233.8 17.1 %psum.144 = f32[64]{0:T(128)S(1)} all-reduce(f32[64]{0:T(128)S(1)} %psum.143), channel_id=1, replica_groups=mesh['tile'=8,'sub'=4] {'tile'}, use_global_device_ids=true, to_apply=%region_17.18 | all-reduce | flops 64 | bytes 512 | tf_op jit(solution)/shard_map/psum | solution.py:16
  250.9 1.9 fusion.78
  254.2 1.6 copy.208
  276.2 3.0 fusion.17
  279.3 3.0 collective-permute-start.33
  282.3 3.9 collective-permute-start.32
  288.3 1.6 scatter-add.61
  290.7 2.9 collective-permute-start.34
  293.6 1.7 copy_add_fusion.1
  297.6 4.9 collective-permute-done.35
  305.0 6.4 %psum.145 = f32[64]{0:T(128)} all-reduce(f32[64]{0:T(128)S(1)} %multiply_reduce_fusion.1), channel_id=1, replica_groups=mesh['tile'=8,'sub'=4] {'sub'}, use_global_device_ids=true, to_apply=%region_19.20 | all-reduce | flops 64 | bytes 512 | tf_op jit(solution)/shard_map/psum | solution.py:15
  311.3 17.2 %psum.146 = f32[64]{0:T(128)S(1)} all-reduce(f32[64]{0:T(128)} %psum.145), channel_id=1, replica_groups=mesh['tile'=8,'sub'=4] {'tile'}, use_global_device_ids=true, to_apply=%region_20.21 | all-reduce | flops 64 | bytes 512 | tf_op jit(solution)/shard_map/psum | solution.py:16
  329.6 2.4 fusion.76
  336.6 1.6 copy.231
  341.4 1.6 copy.228
  356.8 3.0 collective-permute-start.39
  359.9 3.9 collective-permute-start.38
  366.0 2.8 collective-permute-start.40
  371.8 5.2 collective-permute-done.41
  380.3 6.5 %all-reduce.38 = (f32[64]{0:T(128)}, f32[64]{0:T(128)}) all-reduce(f32[64]{0:T(128)} %get-tuple-element.338, f32[64]{0:T(128)S(1)} %multiply_reduce_fusion), channel_id=1, replica_groups=mesh['tile'=8,'sub'=4] {'sub'}, use_global_device_ids=true, to_apply=%region_10.11 | all-reduce | flops 128 | bytes 1024 | tf_op jit(solution)/shard_map/psum | solution.py:15
  386.7 17.5 %psum.148 = f32[64]{0:T(128)S(1)} all-reduce(f32[64]{0:T(128)} %get-tuple-element.214), channel_id=1, replica_groups=mesh['tile'=8,'sub'=4] {'tile'}, use_global_device_ids=true, to_apply=%region_23.24 | all-reduce | flops 64 | bytes 512 | tf_op jit(solution)/shard_map/psum | solution.py:16
  405.3 2.6 fusion.75
  409.0 2.1 convolution_add_fusion.4
  411.2 1.8 fusion.14
  413.3 2.0 add_add_fusion
  419.6 3.0 collective-permute-start.45
  422.6 3.8 collective-permute-start.44
  426.4 4.0 reduce-scatter.10.cloned.1.call-done
  431.4 22.1 %reduce-scatter.8.cloned.1.call-done = f32[64,256]{1,0:T(8,128)} async-done(((f32[64,1024]{1,0:T(8,128)}), f32[64,256]{1,0:T(8,128)}) %reduce-scatter.8.cloned.1.call-update) | async-done | bytes 65552 | tf_op jit(solution)/shard_map/reduce_scatter | solution.py:181
  453.5 36.0 %reduce-scatter.6.cloned.1.call-done = f32[576,256]{1,0:T(8,128)} async-done(((f32[576,1024]{1,0:T(8,128)}), f32[576,256]{1,0:T(8,128)}) %reduce-scatter.6.cloned.1.call-update) | async-done | bytes 589840 | tf_op jit(solution)/shard_map/reduce_scatter | solution.py:180
  489.5 44.4 %all-reduce.41 = (f32[64]{0:T(128)S(1)}, bf16[576,256]{1,0:T(8,128)(2,1)}, bf16[1,256]{1,0:T(2,128)(2,1)S(1)}, bf16[64,256]{1,0:T(8,128)(2,1)S(1)}) all-reduce(f32[64]{0:T(128)S(1)} %copy-done.53, f32[576,256]{1,0:T(8,128)} %reduce-scatter.6.cloned.1.call-done, f32[1,256]{1,0:T(1,128)S(1)} %copy.248, ...), channel_id=1, replica_groups=mesh['tile'=8,'sub'=4] {'tile'}, use_global_device_ids=true, to_apply=%region_11.12 | all-reduce | flops 164160 | bytes 985088 | tf_op jit(solution)/shard_map/psum | solution.py:16
  534.0 1.8 collective-permute-start.46
  537.7 4.5 collective-permute-done.47
  543.0 5.2 all_gather.10
  548.8 5.4 all_gather.11
  555.7 3.0 convert_element_type.174
  (405 shorter events, 134.2 us)
Async XLA Ops:
  7.2 423.2 %reduce-scatter.10.cloned.1.call-start = ((), (), s32[]{:S(2)}) async-start(), calls=%async_computation.6 | async-start | bytes 655360
  8.3 7.6 %collective-permute-start = (bf16[64,8,1]{0,2,1:T(2,128)(2,1)S(1)}, bf16[64,8,1]{0,2,1:T(2,128)(2,1)S(1)}, u32[]{:S(2)}, u32[]{:S(2)}) collective-permute-start(bf16[64,8,1]{0,2,1:T(2,128)(2,1)S(1)} %get-tuple-element.320), channel_id=1, source_target_pairs={{0,4},{4,8},{8,12},{12,16},{16,20},{20,24},{24,28},{28,0},{1,5},{5... | collective-permute-start | bytes 3080 | tf_op jit(solution)/shard_map/ppermute | solution.py:22
  11.3 4.6 collective-permute-start.1
  16.0 10.8 %collective-permute-start.5 = (bf16[64,34]{0,1:T(8,128)(2,1)S(1)}, bf16[64,34]{0,1:T(8,128)(2,1)S(1)}, u32[]{:S(2)}, u32[]{:S(2)}) collective-permute-start(bf16[64,34]{0,1:T(8,128)(2,1)S(1)} %get-tuple-element.312), channel_id=1, source_target_pairs={{1,0},{2,1},{3,2},{5,4},{6,5},{7,6},{9,8},{10,9},{11,10},{13,12},{... | collective-permute-start | bytes 13064 | tf_op jit(solution)/shard_map/ppermute | solution.py:28
  17.3 9.5 %collective-permute-start.4 = (bf16[64,34]{0,1:T(8,128)(2,1)S(1)}, bf16[64,34]{0,1:T(8,128)(2,1)S(1)}, u32[]{:S(2)}, u32[]{:S(2)}) collective-permute-start(bf16[64,34]{0,1:T(8,128)(2,1)S(1)} %get-tuple-element.312), channel_id=1, source_target_pairs={{0,19},{1,20},{2,21},{3,22},{4,23},{5,24},{6,25},{7,26},{8,27},{9,... | collective-permute-start | bytes 13064 | tf_op jit(solution)/shard_map/ppermute | solution.py:22
  23.2 7.2 %collective-permute-start.3 = (bf16[64,34]{0,1:T(8,128)(2,1)S(1)}, bf16[64,34]{0,1:T(8,128)(2,1)S(1)}, u32[]{:S(2)}, u32[]{:S(2)}) collective-permute-start(bf16[64,34]{0,1:T(8,128)(2,1)S(1)} %get-tuple-element.313), channel_id=1, source_target_pairs={{0,1},{1,2},{2,3},{4,5},{5,6},{6,7},{8,9},{9,10},{10,11},{12,13},{... | collective-permute-start | bytes 13064 | tf_op jit(solution)/shard_map/ppermute | solution.py:28
  25.4 4.9 collective-permute-start.2
  33.4 44.0 %copy-start.9 = (bf16[1024,256]{0,1:T(8,128)(2,1)}, bf16[1024,256]{0,1:T(8,128)(2,1)S(1)}, u32[]{:S(2)}) copy-start(bf16[1024,256]{0,1:T(8,128)(2,1)S(1)} %get-tuple-element.324) | copy-start | bytes 1572868
  61.1 6.4 %collective-permute-start.6 = (bf16[64,8,1]{0,2,1:T(2,128)(2,1)S(1)}, bf16[64,8,1]{0,2,1:T(2,128)(2,1)S(1)}, u32[]{:S(2)}, u32[]{:S(2)}) collective-permute-start(bf16[64,8,1]{0,2,1:T(2,128)(2,1)S(1)} %get-tuple-element.318), channel_id=1, source_target_pairs={{0,4},{4,8},{8,12},{12,16},{16,20},{20,24},{24,28},{28,0},{1,5},{5... | collective-permute-start | bytes 3080 | tf_op jit(solution)/shard_map/ppermute | solution.py:22
  61.6 5.8 %collective-permute-start.7 = (bf16[64,8,1]{0,2,1:T(2,128)(2,1)S(1)}, bf16[64,8,1]{0,2,1:T(2,128)(2,1)S(1)}, u32[]{:S(2)}, u32[]{:S(2)}) collective-permute-start(bf16[64,8,1]{0,2,1:T(2,128)(2,1)S(1)} %get-tuple-element.319), channel_id=1, source_target_pairs={{0,28},{4,0},{8,4},{12,8},{16,12},{20,16},{24,20},{28,24},{1,29},{... | collective-permute-start | bytes 3080 | tf_op jit(solution)/shard_map/ppermute | solution.py:22
  67.5 8.3 %collective-permute-start.10 = (bf16[64,34]{0,1:T(8,128)(2,1)S(1)}, bf16[64,34]{0,1:T(8,128)(2,1)S(1)}, u32[]{:S(2)}, u32[]{:S(2)}) collective-permute-start(bf16[64,34]{0,1:T(8,128)(2,1)S(1)} %get-tuple-element.308), channel_id=1, source_target_pairs={{0,19},{1,20},{2,21},{3,22},{4,23},{5,24},{6,25},{7,26},{8,27},{9,... | collective-permute-start | bytes 13064 | tf_op jit(solution)/shard_map/ppermute | solution.py:22
  67.5 8.3 %collective-permute-start.11 = (bf16[64,34]{0,1:T(8,128)(2,1)S(1)}, bf16[64,34]{0,1:T(8,128)(2,1)S(1)}, u32[]{:S(2)}, u32[]{:S(2)}) collective-permute-start(bf16[64,34]{0,1:T(8,128)(2,1)S(1)} %get-tuple-element.308), channel_id=1, source_target_pairs={{1,0},{2,1},{3,2},{5,4},{6,5},{7,6},{9,8},{10,9},{11,10},{13,12},{... | collective-permute-start | bytes 13064 | tf_op jit(solution)/shard_map/ppermute | solution.py:28
  68.8 8.4 %collective-permute-start.9 = (bf16[64,34]{0,1:T(8,128)(2,1)S(1)}, bf16[64,34]{0,1:T(8,128)(2,1)S(1)}, u32[]{:S(2)}, u32[]{:S(2)}) collective-permute-start(bf16[64,34]{0,1:T(8,128)(2,1)S(1)} %get-tuple-element.309), channel_id=1, source_target_pairs={{0,1},{1,2},{2,3},{4,5},{5,6},{6,7},{8,9},{9,10},{10,11},{12,13},{... | collective-permute-start | bytes 13064 | tf_op jit(solution)/shard_map/ppermute | solution.py:28
  71.9 5.3 collective-permute-start.8
  80.2 45.9 %copy-start.10 = (bf16[1024,256]{0,1:T(8,128)(2,1)}, bf16[1024,256]{0,1:T(8,128)(2,1)S(1)}, u32[]{:S(2)}) copy-start(bf16[1024,256]{0,1:T(8,128)(2,1)S(1)} %get-tuple-element.328) | copy-start | bytes 1572868
  80.2 34.5 %copy-start.45 = (f32[1,64,256]{2,1,0:T(8,128)S(1)}, f32[1,64,256]{2,1,0:T(8,128)}, u32[]{:S(2)}) copy-start(f32[1,64,256]{2,1,0:T(8,128)} %param.39) | copy-start | bytes 196612
  109.9 6.4 %collective-permute-start.12 = (bf16[64,8,1]{0,2,1:T(2,128)(2,1)S(1)}, bf16[64,8,1]{0,2,1:T(2,128)(2,1)S(1)}, u32[]{:S(2)}, u32[]{:S(2)}) collective-permute-start(bf16[64,8,1]{0,2,1:T(2,128)(2,1)S(1)} %get-tuple-element.316), channel_id=1, source_target_pairs={{0,4},{4,8},{8,12},{12,16},{16,20},{20,24},{24,28},{28,0},{1,5},{5... | collective-permute-start | bytes 3080 | tf_op jit(solution)/shard_map/ppermute | solution.py:22
  110.0 6.3 %collective-permute-start.13 = (bf16[64,8,1]{0,2,1:T(2,128)(2,1)S(1)}, bf16[64,8,1]{0,2,1:T(2,128)(2,1)S(1)}, u32[]{:S(2)}, u32[]{:S(2)}) collective-permute-start(bf16[64,8,1]{0,2,1:T(2,128)(2,1)S(1)} %get-tuple-element.317), channel_id=1, source_target_pairs={{0,28},{4,0},{8,4},{12,8},{16,12},{20,16},{24,20},{28,24},{1,29},{... | collective-permute-start | bytes 3080 | tf_op jit(solution)/shard_map/ppermute | solution.py:22
  114.8 62.4 %copy-start.2 = (f32[1,64,256]{1,2,0:T(8,128)}, f32[1,64,256]{1,2,0:T(8,128)S(1)}, u32[]{:S(2)}) copy-start(f32[1,64,256]{1,2,0:T(8,128)S(1)} %copy.206) | copy-start | bytes 196612
  116.3 8.2 %collective-permute-start.17 = (bf16[64,34]{0,1:T(8,128)(2,1)S(1)}, bf16[64,34]{0,1:T(8,128)(2,1)S(1)}, u32[]{:S(2)}, u32[]{:S(2)}) collective-permute-start(bf16[64,34]{0,1:T(8,128)(2,1)S(1)} %get-tuple-element.304), channel_id=1, source_target_pairs={{1,0},{2,1},{3,2},{5,4},{6,5},{7,6},{9,8},{10,9},{11,10},{13,12},{... | collective-permute-start | bytes 13064 | tf_op jit(solution)/shard_map/ppermute | solution.py:28
  117.6 6.9 %collective-permute-start.16 = (bf16[64,34]{0,1:T(8,128)(2,1)S(1)}, bf16[64,34]{0,1:T(8,128)(2,1)S(1)}, u32[]{:S(2)}, u32[]{:S(2)}) collective-permute-start(bf16[64,34]{0,1:T(8,128)(2,1)S(1)} %get-tuple-element.304), channel_id=1, source_target_pairs={{0,19},{1,20},{2,21},{3,22},{4,23},{5,24},{6,25},{7,26},{8,27},{9,... | collective-permute-start | bytes 13064 | tf_op jit(solution)/shard_map/ppermute | solution.py:22
  117.7 8.2 %collective-permute-start.15 = (bf16[64,34]{0,1:T(8,128)(2,1)S(1)}, bf16[64,34]{0,1:T(8,128)(2,1)S(1)}, u32[]{:S(2)}, u32[]{:S(2)}) collective-permute-start(bf16[64,34]{0,1:T(8,128)(2,1)S(1)} %get-tuple-element.305), channel_id=1, source_target_pairs={{0,1},{1,2},{2,3},{4,5},{5,6},{6,7},{8,9},{9,10},{10,11},{12,13},{... | collective-permute-start | bytes 13064 | tf_op jit(solution)/shard_map/ppermute | solution.py:28
  120.8 5.1 collective-permute-start.14
  127.3 30.7 %copy-start.39 = (f32[64,8,32]{0,2,1:T(8,128)S(1)}, f32[64,8,32]{0,2,1:T(8,128)}, u32[]{:S(2)}) copy-start(f32[64,8,32]{0,2,1:T(8,128)} %get-tuple-element.222) | copy-start | bytes 196612
  128.9 45.7 %copy-start.12 = (bf16[1024,256]{0,1:T(8,128)(2,1)}, bf16[1024,256]{0,1:T(8,128)(2,1)S(1)}, u32[]{:S(2)}) copy-start(bf16[1024,256]{0,1:T(8,128)(2,1)S(1)} %get-tuple-element.332) | copy-start | bytes 1572868
  129.3 28.7 %copy-start.37 = (f32[256,64]{0,1:T(8,128)}, f32[256,64]{0,1:T(8,128)S(1)}, u32[]{:S(2)}) copy-start(f32[256,64]{0,1:T(8,128)S(1)} %get-tuple-element.335) | copy-start | bytes 196612
  158.0 6.4 %collective-permute-start.18 = (bf16[64,8,1]{0,2,1:T(2,128)(2,1)S(1)}, bf16[64,8,1]{0,2,1:T(2,128)(2,1)S(1)}, u32[]{:S(2)}, u32[]{:S(2)}) collective-permute-start(bf16[64,8,1]{0,2,1:T(2,128)(2,1)S(1)} %get-tuple-element.314), channel_id=1, source_target_pairs={{0,4},{4,8},{8,12},{12,16},{16,20},{20,24},{24,28},{28,0},{1,5},{5... | collective-permute-start | bytes 3080 | tf_op jit(solution)/shard_map/ppermute | solution.py:22
  158.1 6.3 %collective-permute-start.19 = (bf16[64,8,1]{0,2,1:T(2,128)(2,1)S(1)}, bf16[64,8,1]{0,2,1:T(2,128)(2,1)S(1)}, u32[]{:S(2)}, u32[]{:S(2)}) collective-permute-start(bf16[64,8,1]{0,2,1:T(2,128)(2,1)S(1)} %get-tuple-element.315), channel_id=1, source_target_pairs={{0,28},{4,0},{8,4},{12,8},{16,12},{20,16},{24,20},{28,24},{1,29},{... | collective-permute-start | bytes 3080 | tf_op jit(solution)/shard_map/ppermute | solution.py:22
  164.4 8.5 %collective-permute-start.22 = (bf16[64,34]{0,1:T(8,128)(2,1)S(1)}, bf16[64,34]{0,1:T(8,128)(2,1)S(1)}, u32[]{:S(2)}, u32[]{:S(2)}) collective-permute-start(bf16[64,34]{0,1:T(8,128)(2,1)S(1)} %get-tuple-element.300), channel_id=1, source_target_pairs={{0,19},{1,20},{2,21},{3,22},{4,23},{5,24},{6,25},{7,26},{8,27},{9,... | collective-permute-start | bytes 13064 | tf_op jit(solution)/shard_map/ppermute | solution.py:22
  164.5 8.5 %collective-permute-start.23 = (bf16[64,34]{0,1:T(8,128)(2,1)S(1)}, bf16[64,34]{0,1:T(8,128)(2,1)S(1)}, u32[]{:S(2)}, u32[]{:S(2)}) collective-permute-start(bf16[64,34]{0,1:T(8,128)(2,1)S(1)} %get-tuple-element.300), channel_id=1, source_target_pairs={{1,0},{2,1},{3,2},{5,4},{6,5},{7,6},{9,8},{10,9},{11,10},{13,12},{... | collective-permute-start | bytes 13064 | tf_op jit(solution)/shard_map/ppermute | solution.py:28
  165.8 8.6 %collective-permute-start.21 = (bf16[64,34]{0,1:T(8,128)(2,1)S(1)}, bf16[64,34]{0,1:T(8,128)(2,1)S(1)}, u32[]{:S(2)}, u32[]{:S(2)}) collective-permute-start(bf16[64,34]{0,1:T(8,128)(2,1)S(1)} %get-tuple-element.301), channel_id=1, source_target_pairs={{0,1},{1,2},{2,3},{4,5},{5,6},{6,7},{8,9},{9,10},{10,11},{12,13},{... | collective-permute-start | bytes 13064 | tf_op jit(solution)/shard_map/ppermute | solution.py:28
  168.8 5.5 collective-permute-start.20
  200.7 10.5 %collective-permute-start.24 = (f32[64,34]{0,1:T(8,128)S(1)}, f32[64,34]{0,1:T(8,128)S(1)}, u32[]{:S(2)}, u32[]{:S(2)}) collective-permute-start(f32[64,34]{0,1:T(8,128)S(1)} %get-tuple-element.282), channel_id=1, source_target_pairs={{0,19},{1,20},{2,21},{3,22},{4,23},{5,24},{6,25},{7,26},{8,27},{9,... | collective-permute-start | bytes 26120 | tf_op jit(solution)/shard_map/ppermute | solution.py:22
  201.6 9.6 %collective-permute-start.25 = (f32[64,34]{0,1:T(8,128)S(1)}, f32[64,34]{0,1:T(8,128)S(1)}, u32[]{:S(2)}, u32[]{:S(2)}) collective-permute-start(f32[64,34]{0,1:T(8,128)S(1)} %get-tuple-element.283), channel_id=1, source_target_pairs={{1,0},{2,1},{3,2},{5,4},{6,5},{7,6},{9,8},{10,9},{11,10},{13,12},{... | collective-permute-start | bytes 26120 | tf_op jit(solution)/shard_map/ppermute | solution.py:28
  204.9 6.3 %collective-permute-start.27 = (f32[64,34]{0,1:T(8,128)S(1)}, f32[64,34]{0,1:T(8,128)S(1)}, u32[]{:S(2)}, u32[]{:S(2)}) collective-permute-start(f32[64,34]{0,1:T(8,128)S(1)} %get-tuple-element.281), channel_id=1, source_target_pairs={{0,1},{1,2},{2,3},{4,5},{5,6},{6,7},{8,9},{9,10},{10,11},{12,13},{... | collective-permute-start | bytes 26120 | tf_op jit(solution)/shard_map/ppermute | solution.py:28
  208.1 6.4 %collective-permute-start.26 = (f32[64,34]{0,1:T(8,128)S(1)}, f32[64,34]{0,1:T(8,128)S(1)}, u32[]{:S(2)}, u32[]{:S(2)}) collective-permute-start(f32[64,34]{0,1:T(8,128)S(1)} %get-tuple-element.284), channel_id=1, source_target_pairs={{0,13},{1,14},{2,15},{3,16},{4,17},{5,18},{6,19},{7,20},{8,21},{9,... | collective-permute-start | bytes 26120 | tf_op jit(solution)/shard_map/ppermute | solution.py:22
  214.5 6.5 %collective-permute-start.28 = (f32[64,8]{0,1:T(8,128)S(1)}, f32[64,8]{0,1:T(8,128)S(1)}, u32[]{:S(2)}, u32[]{:S(2)}) collective-permute-start(f32[64,8]{0,1:T(8,128)S(1)} %bitcast.528), channel_id=1, source_target_pairs={{0,28},{4,0},{8,4},{12,8},{16,12},{20,16},{24,20},{28,24},{1,29},{... | collective-permute-start | bytes 6152 | tf_op jit(solution)/shard_map/ppermute | solution.py:22
  220.9 6.4 %collective-permute-start.29 = (f32[64,8]{0,1:T(8,128)S(1)}, f32[64,8]{0,1:T(8,128)S(1)}, u32[]{:S(2)}, u32[]{:S(2)}) collective-permute-start(f32[64,8]{0,1:T(8,128)S(1)} %bitcast.526), channel_id=1, source_target_pairs={{0,4},{4,8},{8,12},{12,16},{16,20},{20,24},{24,28},{28,0},{1,5},{5... | collective-permute-start | bytes 6152 | tf_op jit(solution)/shard_map/ppermute | solution.py:22
  274.7 11.5 %collective-permute-start.30 = (f32[64,34]{0,1:T(8,128)S(1)}, f32[64,34]{0,1:T(8,128)S(1)}, u32[]{:S(2)}, u32[]{:S(2)}) collective-permute-start(f32[64,34]{0,1:T(8,128)S(1)} %get-tuple-element.276), channel_id=1, source_target_pairs={{0,19},{1,20},{2,21},{3,22},{4,23},{5,24},{6,25},{7,26},{8,27},{9,... | collective-permute-start | bytes 26120 | tf_op jit(solution)/shard_map/ppermute | solution.py:22
  274.8 11.4 %collective-permute-start.31 = (f32[64,34]{0,1:T(8,128)S(1)}, f32[64,34]{0,1:T(8,128)S(1)}, u32[]{:S(2)}, u32[]{:S(2)}) collective-permute-start(f32[64,34]{0,1:T(8,128)S(1)} %get-tuple-element.277), channel_id=1, source_target_pairs={{1,0},{2,1},{3,2},{5,4},{6,5},{7,6},{9,8},{10,9},{11,10},{13,12},{... | collective-permute-start | bytes 26120 | tf_op jit(solution)/shard_map/ppermute | solution.py:28
  279.3 7.7 %collective-permute-start.33 = (f32[64,34]{0,1:T(8,128)S(1)}, f32[64,34]{0,1:T(8,128)S(1)}, u32[]{:S(2)}, u32[]{:S(2)}) collective-permute-start(f32[64,34]{0,1:T(8,128)S(1)} %get-tuple-element.275), channel_id=1, source_target_pairs={{0,1},{1,2},{2,3},{4,5},{5,6},{6,7},{8,9},{9,10},{10,11},{12,13},{... | collective-permute-start | bytes 26120 | tf_op jit(solution)/shard_map/ppermute | solution.py:28
  282.3 5.4 collective-permute-start.32
  290.7 5.6 collective-permute-start.34
  296.2 6.4 %collective-permute-start.35 = (f32[64,8]{0,1:T(8,128)S(1)}, f32[64,8]{0,1:T(8,128)S(1)}, u32[]{:S(2)}, u32[]{:S(2)}) collective-permute-start(f32[64,8]{0,1:T(8,128)S(1)} %get-tuple-element.296), channel_id=1, source_target_pairs={{0,4},{4,8},{8,12},{12,16},{16,20},{20,24},{24,28},{28,0},{1,5},{5... | collective-permute-start | bytes 6152 | tf_op jit(solution)/shard_map/ppermute | solution.py:22
  354.1 9.7 %collective-permute-start.36 = (f32[64,34]{0,1:T(8,128)S(1)}, f32[64,34]{0,1:T(8,128)S(1)}, u32[]{:S(2)}, u32[]{:S(2)}) collective-permute-start(f32[64,34]{0,1:T(8,128)S(1)} %get-tuple-element.270), channel_id=1, source_target_pairs={{0,19},{1,20},{2,21},{3,22},{4,23},{5,24},{6,25},{7,26},{8,27},{9,... | collective-permute-start | bytes 26120 | tf_op jit(solution)/shard_map/ppermute | solution.py:22
  354.1 9.7 %collective-permute-start.37 = (f32[64,34]{0,1:T(8,128)S(1)}, f32[64,34]{0,1:T(8,128)S(1)}, u32[]{:S(2)}, u32[]{:S(2)}) collective-permute-start(f32[64,34]{0,1:T(8,128)S(1)} %get-tuple-element.271), channel_id=1, source_target_pairs={{1,0},{2,1},{3,2},{5,4},{6,5},{7,6},{9,8},{10,9},{11,10},{13,12},{... | collective-permute-start | bytes 26120 | tf_op jit(solution)/shard_map/ppermute | solution.py:28
  356.8 7.0 %collective-permute-start.39 = (f32[64,34]{0,1:T(8,128)S(1)}, f32[64,34]{0,1:T(8,128)S(1)}, u32[]{:S(2)}, u32[]{:S(2)}) collective-permute-start(f32[64,34]{0,1:T(8,128)S(1)} %get-tuple-element.269), channel_id=1, source_target_pairs={{0,1},{1,2},{2,3},{4,5},{5,6},{6,7},{8,9},{9,10},{10,11},{12,13},{... | collective-permute-start | bytes 26120 | tf_op jit(solution)/shard_map/ppermute | solution.py:28
  359.9 5.5 collective-permute-start.38
  366.0 4.4 collective-permute-start.40
  370.4 6.6 %collective-permute-start.41 = (f32[64,8]{0,1:T(8,128)}, f32[64,8]{0,1:T(8,128)}, u32[]{:S(2)}, u32[]{:S(2)}) collective-permute-start(f32[64,8]{0,1:T(8,128)} %bitcast.132), channel_id=1, source_target_pairs={{0,4},{4,8},{8,12},{12,16},{16,20},{20,24},{24,28},{28,0},{1,5},{5... | collective-permute-start | bytes 6152 | tf_op jit(solution)/shard_map/ppermute | solution.py:22
  409.0 44.5 %reduce-scatter.8.cloned.1.call-start = ((), (), s32[]{:S(2)}) async-start(), calls=%async_computation.5 | async-start | bytes 327680 | tf_op jit(solution)/shard_map/reduce_scatter | solution.py:181
  411.1 78.3 %reduce-scatter.6.cloned.1.call-start = ((), (), s32[]{:S(2)}) async-start(), calls=%async_computation.3 | async-start | bytes 2949120 | tf_op jit(solution)/shard_map/reduce_scatter | solution.py:180
  415.3 140.5 %all-gather.2.cloned.1.call-start = ((), (), s32[]{:S(2)}) async-start(), calls=%async_computation.4 | async-start | bytes 1474560 | tf_op jit(solution)/shard_map/all_gather | solution.py:186
  417.7 71.8 %copy-start.53 = (f32[64]{0:T(128)S(1)}, f32[64]{0:T(128)}, u32[]{:S(2)}) copy-start(f32[64]{0:T(128)} %get-tuple-element.213) | copy-start | bytes 772
  418.0 124.3 %copy-start.4 = (f32[1,64,256]{1,2,0:T(8,128)S(1)}, f32[1,64,256]{1,2,0:T(8,128)}, u32[]{:S(2)}) copy-start(f32[1,64,256]{1,2,0:T(8,128)} %copy-done.2) | copy-start | bytes 196612
  418.0 124.3 %copy-start.5 = (f32[64,8,32]{0,2,1:T(8,128)S(1)}, f32[64,8,32]{0,2,1:T(8,128)}, u32[]{:S(2)}) copy-start(f32[64,8,32]{0,2,1:T(8,128)} %scatter-add.65) | copy-start | bytes 196612
  418.0 124.3 %copy-start.6 = (f32[64,8,32]{0,2,1:T(8,128)S(1)}, f32[64,8,32]{0,2,1:T(8,128)}, u32[]{:S(2)}) copy-start(f32[64,8,32]{0,2,1:T(8,128)} %scatter-add.71) | copy-start | bytes 196612
  418.0 124.3 %copy-start.26 = (f32[64,8,32]{0,2,1:T(8,128)S(1)}, f32[64,8,32]{0,2,1:T(8,128)}, u32[]{:S(2)}) copy-start(f32[64,8,32]{0,2,1:T(8,128)} %copy-done.25) | copy-start | bytes 196612
  418.1 115.8 %collective-permute-start.42 = (f32[64,34]{0,1:T(8,128)S(1)}, f32[64,34]{0,1:T(8,128)S(1)}, u32[]{:S(2)}, u32[]{:S(2)}) collective-permute-start(f32[64,34]{0,1:T(8,128)S(1)} %get-tuple-element.264), channel_id=1, source_target_pairs={{0,19},{1,20},{2,21},{3,22},{4,23},{5,24},{6,25},{7,26},{8,27},{9,... | collective-permute-start | bytes 26120 | tf_op jit(solution)/shard_map/ppermute | solution.py:22
  418.1 115.8 %collective-permute-start.43 = (f32[64,34]{0,1:T(8,128)S(1)}, f32[64,34]{0,1:T(8,128)S(1)}, u32[]{:S(2)}, u32[]{:S(2)}) collective-permute-start(f32[64,34]{0,1:T(8,128)S(1)} %get-tuple-element.265), channel_id=1, source_target_pairs={{1,0},{2,1},{3,2},{5,4},{6,5},{7,6},{9,8},{10,9},{11,10},{13,12},{... | collective-permute-start | bytes 26120 | tf_op jit(solution)/shard_map/ppermute | solution.py:28
  419.6 114.4 %collective-permute-start.45 = (f32[64,34]{0,1:T(8,128)S(1)}, f32[64,34]{0,1:T(8,128)S(1)}, u32[]{:S(2)}, u32[]{:S(2)}) collective-permute-start(f32[64,34]{0,1:T(8,128)S(1)} %get-tuple-element.263), channel_id=1, source_target_pairs={{0,1},{1,2},{2,3},{4,5},{5,6},{6,7},{8,9},{9,10},{10,11},{12,13},{... | collective-permute-start | bytes 26120 | tf_op jit(solution)/shard_map/ppermute | solution.py:28
  422.6 111.3 %collective-permute-start.44 = (f32[64,34]{0,1:T(8,128)S(1)}, f32[64,34]{0,1:T(8,128)S(1)}, u32[]{:S(2)}, u32[]{:S(2)}) collective-permute-start(f32[64,34]{0,1:T(8,128)S(1)} %get-tuple-element.266), channel_id=1, source_target_pairs={{0,13},{1,14},{2,15},{3,16},{4,17},{5,18},{6,19},{7,20},{8,21},{9,... | collective-permute-start | bytes 26120 | tf_op jit(solution)/shard_map/ppermute | solution.py:22
  534.0 3.7 collective-permute-start.46
  535.8 6.4 %collective-permute-start.47 = (f32[64,8]{0,1:T(8,128)S(1)}, f32[64,8]{0,1:T(8,128)S(1)}, u32[]{:S(2)}, u32[]{:S(2)}) collective-permute-start(f32[64,8]{0,1:T(8,128)S(1)} %bitcast.527), channel_id=1, source_target_pairs={{0,4},{4,8},{8,12},{12,16},{16,20},{20,24},{24,28},{28,0},{1,5},{5... | collective-permute-start | bytes 6152 | tf_op jit(solution)/shard_map/ppermute | solution.py:22
  (46 other events, 434.2 us)
Sparse Core Ops, SparseCore 0:
  409.1 21.2 reduce-scatter.9
  433.5 19.9 reduce-scatter.7
  456.6 32.8 reduce-scatter.5
  534.0 15.9 all-gather.1
